TPU v7x, 32 devices: a whole 2x2x4 slice. The times are simulated.
32 devices in a mesh: ga: 8 (over y, x, core), ba: 4 (over z).
Axes of the slice: x: 2, y: 2, z: 4, core: 2. Of those that a mesh axis runs over, the one named last changes fastest.
Arguments:
- psi: float32 [2, 16384, 2048], P(None, 'ga', 'ba'), may hold values from -0.1875 to 0.1875
- dpsi: float32 [2, 16384, 512], P(None, 'ga', 'ba'), may hold values from -6 to 6
- band_weight: float32 [2048], replicated, may hold values from 0.25 to 1
- panel_band: int32 [16], P('ba'), may hold values from 0 to 15, each once
- slab_offset: int32 [8], replicated, may hold values from 0 to 2047
Outputs:
- projected: float32 [2, 16384, 512], P(None, 'ga', 'ba')
Inputs may be any that keep to these rules, and one draw needn't show every extreme that they name: panel_band is a permutation of the panel numbers.
All inputs are finite; a program needn't handle non-finite values.
Results may differ from a plain program's by a relative error of at most 0.00012.
Values sent between devices are 32-bit elements; how exact they have to be, the bound alone decides.
A program may use at most 128 MiB of HBM per device.

v0:
```python
import jax
import jax.numpy as jnp
from jax import lax
from jax.sharding import PartitionSpec as P

PANEL = 128


def tdot(left, right):
    return lax.dot_general(
        left,
        right,
        (((0,), (0,)), ((), ())),
        precision=lax.Precision.HIGHEST,
        preferred_element_type=jnp.float32,
    )


def mdot(left, right):
    return jnp.dot(left, right, precision=lax.Precision.HIGHEST, preferred_element_type=jnp.float32)


def margin_of(waves, columns):
    over_re = tdot(waves[0], columns[0]) + tdot(waves[1], columns[1])
    over_im = tdot(waves[0], columns[1]) - tdot(waves[1], columns[0])
    return jnp.stack([over_re, over_im])


def correct_with(waves, weighted):
    corr_re = mdot(waves[0], weighted[0]) - mdot(waves[1], weighted[1])
    corr_im = mdot(waves[0], weighted[1]) + mdot(waves[1], weighted[0])
    return jnp.stack([corr_re, corr_im])


def weights_for(band_weight, panels):
    table = band_weight.reshape(-1, PANEL)
    onehot = (panels[:, None] == jnp.arange(table.shape[0], dtype=jnp.int32)[None, :]).astype(
        jnp.float32
    )
    return mdot(onehot, table).reshape(-1)


def per_device(psi, dpsi, band_weight, panel_band, slab_offset):
    offset = slab_offset[lax.axis_index("ga")]
    aligned = jnp.roll(dpsi, -offset, axis=1)
    local_weight = weights_for(band_weight, panel_band)
    blocks = margin_of(psi, lax.all_gather(aligned, "ba", axis=2, tiled=True))
    margin = lax.psum(blocks, "ga")
    weighted = margin * local_weight[None, :, None]
    correction = correct_with(psi, weighted)
    share = lax.psum_scatter(correction, "ba", scatter_dimension=2, tiled=True)
    result = aligned - share
    return jnp.roll(result, offset, axis=1)


def solution(mesh):
    in_specs = (P(None, "ga", "ba"), P(None, "ga", "ba"), P(), P("ba"), P())
    out_specs = P(None, "ga", "ba")
    return jax.shard_map(
        per_device, mesh=mesh, in_specs=in_specs, out_specs=out_specs, check_vma=False
    )
```

profile of v0, /device:TPU:0, one launch (start us, length us, event | category | flops | bytes accessed | tf_op | source)
XLA Modules:
  0.0 466.1 jit_solution(3996148815091841346)
XLA Ops:
  6.5 1.3 dynamic_slice.6
  9.1 1.9 copy.6
  11.0 2.5 fusion.29
  13.5 0.0 all-gather.2.cloned.1.call-update
  13.5 0.0 all-reduce.2.cloned.1.call-start
  13.6 152.4 %all-gather.2.cloned.1.call-done = f32[2,2048,512]{1,2,0:T(8,128)} async-done(((f32[2,2048,128]{1,2,0:T(8,128)}), f32[2,2048,512]{1,2,0:T(8,128)}) %all-gather.2.cloned.1.call-update) | async-done | bytes 8388624 | tf_op jit(solution)/shard_map/all_gather | solution.py:47
  166.0 9.4 %fusion.4 = f32[512,512]{1,0:T(8,128)S(1)} fusion(f32[2,2048,512]{1,2,0:T(8,128)} %all-gather.2.cloned.1.call-done, f32[2,2048,512]{2,1,0:T(8,128)} %param.7), kind=kOutput, calls=%fused_computation.11 | convolution fusion | flops 6442450944 | bytes 9437184 | tf_op jit(solution)/shard_map/dot_general | solution.py:10
  175.5 21.7 %fusion.6 = f32[512,512]{1,0:T(8,128)S(1)} fusion(f32[2,2048,512]{1,2,0:T(8,128)} %all-gather.2.cloned.1.call-done, f32[2,2048,512]{2,1,0:T(8,128)} %param.7), kind=kOutput, calls=%fused_computation.13 | convolution fusion | flops 6442450944 | bytes 9437184 | tf_op jit(solution)/shard_map/dot_general | solution.py:10
  197.3 6.8 %fusion.39 = f32[1,512,512]{1,2,0:T(8,128)S(1)} fusion(f32[512,512]{1,0:T(8,128)S(1)} %fusion.4, f32[2,2048,512]{2,1,0:T(8,128)S(1)} %bitcast.77, f32[2,2048,512]{1,2,0:T(8,128)S(1)} %bitcast.81), kind=kOutput, calls=%fused_computation.39 | convolution fusion | flops 6442713088 | bytes 10485760 | tf_op jit(solution)/shard_map/dot_general | solution.py:10
  204.1 6.8 %fusion.33 = f32[1,512,512]{1,2,0:T(8,128)S(1)} fusion(f32[512,512]{1,0:T(8,128)S(1)} %fusion.6, f32[2,2048,512]{2,1,0:T(8,128)S(1)} %bitcast.77, f32[2,2048,512]{1,2,0:T(8,128)S(1)} %bitcast.81), kind=kOutput, calls=%fused_computation.37 | convolution fusion | flops 6442713088 | bytes 10485760 | tf_op jit(solution)/shard_map/dot_general | solution.py:10
  211.0 1.5 pad_maximum_fusion.1
  212.5 0.0 reduce-scatter.2.cloned.1.call-start
  212.6 0.2 convolution_bitcast_fusion
  212.8 59.8 %all-reduce.2.cloned.1.call-done = f32[2,512,512]{1,2,0:T(8,128)} async-done(((f32[2,512,512]{1,2,0:T(8,128)}), f32[2,512,512]{1,2,0:T(8,128)}) %all-reduce.2.cloned.1.call-update) | async-done | bytes 2097168 | tf_op jit(solution)/shard_map/psum | solution.py:48
  272.6 2.0 broadcast_multiply_fusion
  274.6 9.4 %fusion = f32[512,2048]{1,0:T(8,128)S(1)} fusion(f32[2,2048,512]{2,1,0:T(8,128)} %param.7, f32[2,512,512]{1,2,0:T(8,128)S(1)} %broadcast_multiply_fusion), kind=kOutput, calls=%fused_computation.7 | convolution fusion | flops 6442450944 | bytes 9437184 | tf_op jit(solution)/shard_map/dot_general | solution.py:20
  284.1 7.2 %fusion.2 = f32[512,2048]{1,0:T(8,128)S(1)} fusion(f32[2,2048,512]{2,1,0:T(8,128)S(1)} %bitcast.79, f32[2,512,512]{1,2,0:T(8,128)S(1)} %broadcast_multiply_fusion), kind=kOutput, calls=%fused_computation.9 | convolution fusion | flops 6442450944 | bytes 9437184 | tf_op jit(solution)/shard_map/dot_general | solution.py:20
  291.3 7.4 %add_bitcast_fusion = f32[1,2048,512]{1,2,0:T(8,128)S(1)} fusion(f32[512,2048]{1,0:T(8,128)S(1)} %fusion, f32[2,2048,512]{2,1,0:T(8,128)S(1)} %bitcast.79, f32[2,512,512]{1,2,0:T(8,128)S(1)} %broadcast_multiply_fusion), kind=kOutput, calls=%fused_computation.23 | convolution fusion | flops 6443499520 | bytes 13631488 | tf_op jit(solution)/shard_map/dot_general | solution.py:20
  298.7 7.2 %subtract_bitcast_fusion = f32[1,2048,512]{1,2,0:T(8,128)S(1)} fusion(f32[512,2048]{1,0:T(8,128)S(1)} %fusion.2, f32[2,2048,512]{2,1,0:T(8,128)S(1)} %bitcast.79, f32[2,512,512]{1,2,0:T(8,128)S(1)} %broadcast_multiply_fusion), kind=kOutput, calls=%fused_computation.24 | convolution fusion | flops 6443499520 | bytes 13631488 | tf_op jit(solution)/shard_map/dot_general | solution.py:20
  306.0 3.8 pad_maximum_fusion
  311.1 142.6 %reduce-scatter.2.cloned.1.call-done = f32[2,2048,128]{1,2,0:T(8,128)} async-done(((f32[2,2048,512]{1,2,0:T(8,128)}), f32[2,2048,128]{1,2,0:T(8,128)}) %reduce-scatter.2.cloned.1.call-update) | async-done | bytes 2097168 | tf_op jit(solution)/shard_map/reduce_scatter | solution.py:51
  453.7 2.8 fusion.44
  456.4 1.2 fusion.28
  457.6 1.8 copy.8
  (24 shorter events, 0.1 us)
Async XLA Ops:
  6.5 206.0 %copy-start = (f32[2048]{0:T(1024)S(1)}, f32[2048]{0:T(1024)}, u32[]{:S(2)}) copy-start(f32[2048]{0:T(1024)} %param.9) | copy-start | bytes 24580
  6.5 159.5 %all-gather.2.cloned.1.call-start = ((), (), s32[]{:S(2)}) async-start(), calls=%async_computation.1 | async-start | bytes 10485760 | tf_op jit(solution)/shard_map/all_gather | solution.py:47
  13.5 259.0 %all-reduce.2.cloned.1.call-start = ((), (), s32[]{:S(2)}) async-start(), calls=%async_computation.2 | async-start | bytes 4194304 | tf_op jit(solution)/shard_map/psum | solution.py:48
  166.0 31.2 %slice-start = ((s8[8388608]{0:T(1024)(128)(4,1)}), s8[4194304]{0:T(1024)(128)(4,1)S(1)}, s32[]{:S(2)}) async-start(s8[8388608]{0:T(1024)(128)(4,1)} %bitcast.76), calls=%async_computation.4 | async-start | bytes 8388608
  166.0 31.2 %slice-start.4 = ((s8[8388608]{0:T(1024)(128)(4,1)}), s8[4194304]{0:T(1024)(128)(4,1)S(1)}, s32[]{:S(2)}) async-start(s8[8388608]{0:T(1024)(128)(4,1)} %bitcast.80), calls=%async_computation.8 | async-start | bytes 8388608
  175.5 21.7 %slice-start.1 = ((s8[8388608]{0:T(1024)(128)(4,1)}), s8[4194304]{0:T(1024)(128)(4,1)S(1)}, s32[]{:S(2)}) async-start(s8[8388608]{0:T(1024)(128)(4,1)} %bitcast.76), calls=%async_computation.5 | async-start | bytes 8388608
  175.5 21.7 %slice-start.5 = ((s8[8388608]{0:T(1024)(128)(4,1)}), s8[4194304]{0:T(1024)(128)(4,1)S(1)}, s32[]{:S(2)}) async-start(s8[8388608]{0:T(1024)(128)(4,1)} %bitcast.80), calls=%async_computation.9 | async-start | bytes 8388608
  211.0 1.6 copy-start.2
  212.5 241.2 %reduce-scatter.2.cloned.1.call-start = ((), (), s32[]{:S(2)}) async-start(), calls=%async_computation.3 | async-start | bytes 10485760 | tf_op jit(solution)/shard_map/reduce_scatter | solution.py:51
  272.6 11.5 %slice-start.2 = ((s8[8388608]{0:T(1024)(128)(4,1)}), s8[4194304]{0:T(1024)(128)(4,1)S(1)}, s32[]{:S(2)}) async-start(s8[8388608]{0:T(1024)(128)(4,1)} %bitcast.78), calls=%async_computation.6 | async-start | bytes 8388608
  274.6 9.5 %slice-start.3 = ((s8[8388608]{0:T(1024)(128)(4,1)}), s8[4194304]{0:T(1024)(128)(4,1)S(1)}, s32[]{:S(2)}) async-start(s8[8388608]{0:T(1024)(128)(4,1)} %bitcast.78), calls=%async_computation.7 | async-start | bytes 8388608
  453.7 5.7 %copy-start.1 = (f32[2048]{0:T(1024)S(1)}, f32[2048]{0:T(1024)}, u32[]{:S(2)}) copy-start(f32[2048]{0:T(1024)} %param.9) | copy-start | bytes 24580
Sparse Core Ops, SparseCore 0:
  13.7 152.3 all-gather.1
  212.6 59.9 all-reduce.1
  309.9 143.6 reduce-scatter.1
where the time goes:
time: 472 us; the launch traced here: 466 us
  waiting for transfers between devices  355 us (75%)
  matrix products  76.3 us (16%)
  between operations  16 us (3%)
  other arithmetic  13.7 us (3%)
  local copies, waits for them, and re-layouts  5.08 us (1%)
    all_gather x1, waiting for transfers between devices, per_device(): blocks = margin_of(psi, lax.all_gather(aligned, 'ba', axis=2, tiled=True))  152 us
    reduce_scatter x1, waiting for transfers between devices, per_device(): share = lax.psum_scatter(correction, 'ba', scatter_dimension=2, tiled=True)  143 us
    psum x1, waiting for transfers between devices, per_device(): margin = lax.psum(blocks, 'ga')  59.8 us
    dot_general x4, matrix products, tdot(): lax.dot_general(left, right, (((0,), (0,)), ((), ())), precision=lax.Prec...  44.8 us
    dot_general x5, matrix products, mdot(): jnp.dot(left, right, precision=lax.Precision.HIGHEST, preferred_element_t...  31.5 us
  transfers between devices with their start and end apart: 3, of which 3 were waited for; matrix products, arithmetic and copies ran while one was open for 0% of the time, Pallas kernels for 0%

commit v1 on v0

--- a/solution.py
+++ b/solution.py
@@ -45,7 +45,10 @@
     aligned = jnp.roll(dpsi, -offset, axis=1)
     local_weight = weights_for(band_weight, panel_band)
     blocks = margin_of(psi, lax.all_gather(aligned, "ba", axis=2, tiled=True))
-    margin = lax.psum(blocks, "ga")
+    slots = lax.axis_size("ga")
+    margin = blocks
+    for k in [[(u, u ^ i0) for u in range(slots)] for i0 in (1, 2, 4, 8, 16) if i0 < slots]:
+        margin = margin + lax.ppermute(margin, "ga", k)
     weighted = margin * local_weight[None, :, None]
     correction = correct_with(psi, weighted)
     share = lax.psum_scatter(correction, "ba", scatter_dimension=2, tiled=True)

time: 472 us -> 496 us (1.051)
  waiting for transfers between devices: 355 us -> 390 us
  matrix products: 76.3 us -> 63.1 us
    ppermute x0 -> x3, waiting for transfers between devices: none -> 95.5 us  [per_device(): margin = margin + lax.ppermute(margin, 'ga', k)]
    psum x1 -> x0, waiting for transfers between devices: 59.8 us -> none  [per_device(): margin = lax.psum(blocks, 'ga')]
    dot_general x4, matrix products: 44.8 us -> 33.5 us  [tdot(): lax.dot_general(left, right, (((0,), (0,)), ((), ())), precision=lax.Prec...]
  transfers between devices with their start and end apart: 3 -> 5, of which waited for: 3 -> 5; matrix products, arithmetic and copies ran while one was open for 0% -> 0% of each run, Pallas kernels for 0% -> 0%
where the time goes in v1:
time: 496 us; the launch traced here: 490 us
  waiting for transfers between devices  390 us (79%)
  matrix products  63.1 us (13%)
  between operations  16.3 us (3%)
  other arithmetic  12.3 us (2%)
  local copies, waits for them, and re-layouts  5.04 us (1%)
    all_gather x1, waiting for transfers between devices, per_device(): blocks = margin_of(psi, lax.all_gather(aligned, 'ba', axis=2, tiled=True))  152 us
    reduce_scatter x1, waiting for transfers between devices, per_device(): share = lax.psum_scatter(correction, 'ba', scatter_dimension=2, tiled=True)  142 us
    ppermute x3, waiting for transfers between devices, per_device(): margin = margin + lax.ppermute(margin, 'ga', k)  95.5 us
    dot_general x4, matrix products, tdot(): lax.dot_general(left, right, (((0,), (0,)), ((), ())), precision=lax.Prec...  33.5 us
    dot_general x5, matrix products, mdot(): jnp.dot(left, right, precision=lax.Precision.HIGHEST, preferred_element_t...  29.6 us
  transfers between devices with their start and end apart: 5, of which 5 were waited for; matrix products, arithmetic and copies ran while one was open for 0% of the time, Pallas kernels for 0%

profile of v1, /device:TPU:0, one launch (start us, length us, event | category | flops | bytes accessed | tf_op | source)
XLA Modules:
  0.0 489.6 jit_solution(3209374711186903793)
XLA Ops:
  6.5 1.3 dynamic_slice.6
  9.1 1.9 copy.6
  11.0 2.5 fusion.29
  13.6 152.4 %all-gather.2.cloned.1.call-done = f32[2,2048,512]{1,2,0:T(8,128)} async-done(((f32[2,2048,128]{1,2,0:T(8,128)}), f32[2,2048,512]{1,2,0:T(8,128)}) %all-gather.2.cloned.1.call-update) | async-done | bytes 8388624 | tf_op jit(solution)/shard_map/all_gather | solution.py:47
  166.0 9.5 %fusion.4 = f32[512,512]{1,0:T(8,128)S(1)} fusion(f32[2,2048,512]{1,2,0:T(8,128)} %all-gather.2.cloned.1.call-done, f32[2,2048,512]{2,1,0:T(8,128)} %param.7), kind=kOutput, calls=%fused_computation.11 | convolution fusion | flops 6442450944 | bytes 9437184 | tf_op jit(solution)/shard_map/dot_general | solution.py:10
  175.5 10.3 %fusion.6 = f32[512,512]{1,0:T(8,128)S(1)} fusion(f32[2,2048,512]{1,2,0:T(8,128)} %all-gather.2.cloned.1.call-done, f32[2,2048,512]{2,1,0:T(8,128)} %param.7), kind=kOutput, calls=%fused_computation.13 | convolution fusion | flops 6442450944 | bytes 9437184 | tf_op jit(solution)/shard_map/dot_general | solution.py:10
  185.9 6.8 %fusion.39 = f32[1,512,512]{1,2,0:T(8,128)S(1)} fusion(f32[512,512]{1,0:T(8,128)S(1)} %fusion.4, f32[2,2048,512]{2,1,0:T(8,128)S(1)} %bitcast.77, f32[2,2048,512]{1,2,0:T(8,128)S(1)} %bitcast.79), kind=kOutput, calls=%fused_computation.40 | convolution fusion | flops 6442713088 | bytes 10485760 | tf_op jit(solution)/shard_map/dot_general | solution.py:10
  192.8 6.8 %fusion.33 = f32[1,512,512]{1,2,0:T(8,128)S(1)} fusion(f32[512,512]{1,0:T(8,128)S(1)} %fusion.6, f32[2,2048,512]{2,1,0:T(8,128)S(1)} %bitcast.77, f32[2,2048,512]{1,2,0:T(8,128)S(1)} %bitcast.79), kind=kOutput, calls=%fused_computation.38 | convolution fusion | flops 6442713088 | bytes 10485760 | tf_op jit(solution)/shard_map/dot_general | solution.py:10
  199.9 4.1 collective-permute-done
  204.0 0.7 fusion.44
  204.7 1.5 collective-permute-start.1
  206.3 46.2 %collective-permute-done.1 = f32[2,512,512]{1,2,0:T(8,128)S(1)} collective-permute-done((f32[2,512,512]{1,2,0:T(8,128)S(1)}, f32[2,512,512]{1,2,0:T(8,128)S(1)}, u32[]{:S(2)}, u32[]{:S(2)}) %collective-permute-start.1) | collective-permute-done | bytes 2097184 | tf_op jit(solution)/shard_map/ppermute | solution.py:51
  252.5 0.8 fusion.46
  253.2 1.5 collective-permute-start.2
  254.9 45.2 %collective-permute-done.2 = f32[2,512,512]{1,2,0:T(8,128)S(1)} collective-permute-done((f32[2,512,512]{1,2,0:T(8,128)S(1)}, f32[2,512,512]{1,2,0:T(8,128)S(1)}, u32[]{:S(2)}, u32[]{:S(2)}) %collective-permute-start.2) | collective-permute-done | bytes 2097184 | tf_op jit(solution)/shard_map/ppermute | solution.py:51
  300.6 7.2 %fusion = f32[512,2048]{1,0:T(8,128)S(1)} fusion(f32[2,2048,512]{2,1,0:T(8,128)S(1)} %bitcast.77, f32[2,512,512]{1,2,0:T(8,128)S(1)} %add_multiply_fusion), kind=kOutput, calls=%fused_computation.7 | convolution fusion | flops 6442450944 | bytes 9437184 | tf_op jit(solution)/shard_map/dot_general | solution.py:20
  307.8 7.6 %fusion.2 = f32[512,2048]{1,0:T(8,128)S(1)} fusion(f32[2,2048,512]{2,1,0:T(8,128)S(1)} %bitcast.77, f32[2,512,512]{1,2,0:T(8,128)S(1)} %add_multiply_fusion), kind=kOutput, calls=%fused_computation.9 | convolution fusion | flops 6442450944 | bytes 9437184 | tf_op jit(solution)/shard_map/dot_general | solution.py:20
  315.4 7.2 %add_bitcast_fusion = f32[1,2048,512]{1,2,0:T(8,128)S(1)} fusion(f32[512,2048]{1,0:T(8,128)S(1)} %fusion, f32[2,2048,512]{2,1,0:T(8,128)S(1)} %bitcast.77, f32[2,512,512]{1,2,0:T(8,128)S(1)} %add_multiply_fusion), kind=kOutput, calls=%fused_computation.23 | convolution fusion | flops 6443499520 | bytes 13631488 | tf_op jit(solution)/shard_map/dot_general | solution.py:20
  322.6 7.4 %subtract_bitcast_fusion = f32[1,2048,512]{1,2,0:T(8,128)S(1)} fusion(f32[512,2048]{1,0:T(8,128)S(1)} %fusion.2, f32[2,2048,512]{2,1,0:T(8,128)S(1)} %bitcast.77, f32[2,512,512]{1,2,0:T(8,128)S(1)} %add_multiply_fusion), kind=kOutput, calls=%fused_computation.24 | convolution fusion | flops 6443499520 | bytes 13631488 | tf_op jit(solution)/shard_map/dot_general | solution.py:20
  330.1 3.8 pad_maximum_fusion
  335.2 141.7 %reduce-scatter.2.cloned.1.call-done = f32[2,2048,128]{1,2,0:T(8,128)} async-done(((f32[2,2048,512]{1,2,0:T(8,128)}), f32[2,2048,128]{1,2,0:T(8,128)}) %reduce-scatter.2.cloned.1.call-update) | async-done | bytes 2097168 | tf_op jit(solution)/shard_map/reduce_scatter | solution.py:54
  476.9 2.8 fusion.45
  479.6 1.2 fusion.28
  480.8 1.8 copy.8
  (24 shorter events, 1.0 us)
Async XLA Ops:
  6.5 248.2 %copy-start = (f32[2048]{0:T(1024)S(1)}, f32[2048]{0:T(1024)}, u32[]{:S(2)}) copy-start(f32[2048]{0:T(1024)} %param.9) | copy-start | bytes 24580
  6.5 159.5 %all-gather.2.cloned.1.call-start = ((), (), s32[]{:S(2)}) async-start(), calls=%async_computation.1 | async-start | bytes 10485760 | tf_op jit(solution)/shard_map/all_gather | solution.py:47
  13.5 463.3 %reduce-scatter.2.cloned.1.call-start = ((), (), s32[]{:S(2)}) async-start(), calls=%async_computation.2 | async-start | bytes 10485760 | tf_op jit(solution)/shard_map/reduce_scatter | solution.py:54
  166.0 19.8 %slice-start = ((s8[8388608]{0:T(1024)(128)(4,1)}), s8[4194304]{0:T(1024)(128)(4,1)S(1)}, s32[]{:S(2)}) async-start(s8[8388608]{0:T(1024)(128)(4,1)} %bitcast.76), calls=%async_computation.3 | async-start | bytes 8388608
  166.0 19.8 %slice-start.2 = ((s8[8388608]{0:T(1024)(128)(4,1)}), s8[4194304]{0:T(1024)(128)(4,1)S(1)}, s32[]{:S(2)}) async-start(s8[8388608]{0:T(1024)(128)(4,1)} %bitcast.78), calls=%async_computation.5 | async-start | bytes 8388608
  175.5 10.4 %slice-start.1 = ((s8[8388608]{0:T(1024)(128)(4,1)}), s8[4194304]{0:T(1024)(128)(4,1)S(1)}, s32[]{:S(2)}) async-start(s8[8388608]{0:T(1024)(128)(4,1)} %bitcast.76), calls=%async_computation.4 | async-start | bytes 8388608
  175.5 10.4 %slice-start.3 = ((s8[8388608]{0:T(1024)(128)(4,1)}), s8[4194304]{0:T(1024)(128)(4,1)S(1)}, s32[]{:S(2)}) async-start(s8[8388608]{0:T(1024)(128)(4,1)} %bitcast.78), calls=%async_computation.6 | async-start | bytes 8388608
  199.8 4.2 collective-permute-start
  204.7 50.0 %copy-start.2 = (s32[4]{0:T(128)S(1)}, s32[4]{0:T(128)}, u32[]{:S(2)}) copy-start(s32[4]{0:T(128)} %param.10) | copy-start | bytes 52
  204.7 47.7 %collective-permute-start.1 = (f32[2,512,512]{1,2,0:T(8,128)S(1)}, f32[2,512,512]{1,2,0:T(8,128)S(1)}, u32[]{:S(2)}, u32[]{:S(2)}) collective-permute-start(f32[2,512,512]{1,2,0:T(8,128)S(1)} %fusion.44), channel_id=1, source_target_pairs={{0,8},{4,12},{8,0},{12,4},{16,24},{20,28},{24,16},{28,20},{1,9},{5... | collective-permute-start | bytes 6291464 | tf_op jit(solution)/shard_map/ppermute | solution.py:51
  253.2 46.9 %collective-permute-start.2 = (f32[2,512,512]{1,2,0:T(8,128)S(1)}, f32[2,512,512]{1,2,0:T(8,128)S(1)}, u32[]{:S(2)}, u32[]{:S(2)}) collective-permute-start(f32[2,512,512]{1,2,0:T(8,128)S(1)} %fusion.46), channel_id=1, source_target_pairs={{0,16},{4,20},{8,24},{12,28},{16,0},{20,4},{24,8},{28,12},{1,17},{... | collective-permute-start | bytes 6291464 | tf_op jit(solution)/shard_map/ppermute | solution.py:51
  476.9 5.7 %copy-start.1 = (f32[2048]{0:T(1024)S(1)}, f32[2048]{0:T(1024)}, u32[]{:S(2)}) copy-start(f32[2048]{0:T(1024)} %param.9) | copy-start | bytes 24580
Sparse Core Ops, SparseCore 0:
  13.7 152.3 all-gather.1
  334.0 142.7 reduce-scatter.1
